TPU v7x, 32 devices: a whole 2x2x4 slice. The times are simulated.
32 devices in a mesh: state: 32 (over z, y, x, core).
Axes of the slice: x: 2, y: 2, z: 4, core: 2. Of those that a mesh axis runs over, the one named last changes fastest.
Arguments:
- transitions: float32 [4096, 16, 4096], P('state'), may hold values from 0 to 1, as said below
- costs: float32 [4096, 16, 128], P('state'), may hold values from 0 to 4
- valid_counts: int32 [4096], P('state'), may hold values from 1 to 16
- start_values: float32 [4096, 128], P('state'), may hold values from -12 to 12
- ref_state: int32 [1], replicated, may hold values from 0 to 4095
Outputs:
- relative_values: float32 [4096, 128], P('state')
- lower_bounds: float32 [4, 128], replicated
- upper_bounds: float32 [4, 128], replicated
Inputs may be any that keep to these rules, and one draw needn't show every extreme that they name: Every entry is nonnegative and each row transitions[s, a, :] sums to one up to float32 rounding. Actions 0 to valid_counts[s] - 1 are allowed in state s.
All inputs are finite; a program needn't handle non-finite values.
Results may differ from a plain program's by a relative error of at most 0.00017.
Values sent between devices are 32-bit elements; how exact they have to be, the bound alone decides.
A program may use at most 64 MiB of HBM per device.

v0:
```python
import jax
import jax.numpy as jnp
from jax import lax
from jax.sharding import PartitionSpec as P

ITERS = 4


big_value = 1e30


def local(transitions, costs, valid_counts, start_values, ref_state):
    local_states = transitions.shape[0]
    actions = transitions.shape[1]
    scenarios = start_values.shape[1]
    flat_rows = transitions.reshape(local_states * actions, transitions.shape[2])
    allowed = jnp.arange(actions, dtype=jnp.int32)[None, :] < valid_counts[:, None]
    my_index = lax.axis_index("state")
    first_state = my_index * local_states
    owner_index = ref_state[0] // local_states
    offset = jnp.clip(ref_state[0] - first_state, 0, local_states - 1)
    is_owner = owner_index == my_index
    lower_list = []
    upper_list = []
    unshifted = start_values
    for iteration in range(ITERS):
        field_all = lax.all_gather(unshifted, "state", axis=0, tiled=True)
        bellman_expected = jnp.dot(
            flat_rows,
            field_all,
            precision=lax.Precision.HIGHEST,
            preferred_element_type=jnp.float32,
        )
        q_values = costs + bellman_expected.reshape(local_states, actions, scenarios)
        q_values = jnp.where(allowed[:, :, None], q_values, jnp.float32(big_value))
        best_value = jnp.min(q_values, axis=1)
        increase = best_value - unshifted
        lower_list.append(jnp.min(increase, axis=0))
        upper_list.append(jnp.max(increase, axis=0))
        unshifted = best_value
    local_row = lax.dynamic_slice_in_dim(unshifted, offset, 1, 0)
    masked_row = jnp.where(is_owner, local_row, jnp.float32(-big_value))
    ref_row, upper_all, negated_all = lax.pmax(
        (masked_row, jnp.stack(upper_list), -jnp.stack(lower_list)), "state"
    )
    return (unshifted - ref_row, -negated_all, upper_all)


def solution(mesh):
    in_specs = (P("state", None, None), P("state", None, None), P("state"), P("state", None), P())
    out_specs = (P("state", None), P(), P())
    return jax.shard_map(local, mesh=mesh, in_specs=in_specs, out_specs=out_specs, check_vma=False)
```

profile of v0, /device:TPU:0, one launch (start us, length us, event | category | flops | bytes accessed | tf_op | source)
XLA Modules:
  0.0 436.8 jit_solution(7266139124346158059)
XLA Ops:
  7.2 0.0 all-gather.5.cloned.1.call-start
  7.2 0.7 all-gather.5.cloned.1.call-update
  7.9 0.0 all-gather.7.cloned.1.call-start
  7.9 0.7 iota_compare_fusion
  8.6 0.0 copy-start
  8.6 61.2 %all-gather.5.cloned.1.call-done = f32[4096,128]{1,0:T(8,128)} async-done(((f32[128,128]{1,0:T(8,128)}), f32[4096,128]{1,0:T(8,128)}) %all-gather.5.cloned.1.call-update) | async-done | bytes 2097168 | tf_op jit(solution)/shard_map/all_gather | solution.py:27
  69.8 31.6 %fusion = f32[128,16,128]{2,1,0:T(8,128)S(1)} fusion(f32[128,16,4096]{2,1,0:T(8,128)} %param.5, f32[4096,128]{1,0:T(8,128)} %all-gather.5.cloned.1.call-done), kind=kOutput, calls=%fused_computation.3 | convolution fusion | flops 12884901888 | bytes 36700160 | tf_op jit(solution)/shard_map/dot_general | solution.py:28
  101.4 0.0 copy-done
  101.4 1.3 fusion.3
  102.8 0.0 all-gather.7.cloned.1.call-update
  102.8 0.2 all-gather.9.cloned.1.call-start
  103.0 55.0 %all-gather.7.cloned.1.call-done = f32[4096,128]{1,0:T(8,128)} async-done(((f32[128,128]{1,0:T(8,128)}), f32[4096,128]{1,0:T(8,128)}) %all-gather.7.cloned.1.call-update) | async-done | bytes 2097168 | tf_op jit(solution)/shard_map/all_gather | solution.py:27
  158.0 39.2 %convolution_bitcast_fusion.2 = f32[2048,128]{0,1:T(8,128)S(1)} fusion(f32[4096,128]{1,0:T(8,128)} %all-gather.7.cloned.1.call-done, f32[2048,4096]{1,0:T(8,128)} %bitcast.36), kind=kOutput, calls=%fused_computation.2 | convolution fusion | flops 12884901888 | bytes 36700160 | tf_op jit(solution)/shard_map/dot_general | solution.py:28
  197.2 0.3 copy.15
  197.5 1.3 fusion.9
  198.8 0.0 all-gather.9.cloned.1.call-update
  198.9 0.3 all-gather.11.cloned.1.call-start
  199.1 54.9 %all-gather.9.cloned.1.call-done = f32[4096,128]{1,0:T(8,128)} async-done(((f32[128,128]{1,0:T(8,128)}), f32[4096,128]{1,0:T(8,128)}) %all-gather.9.cloned.1.call-update) | async-done | bytes 2097168 | tf_op jit(solution)/shard_map/all_gather | solution.py:27
  254.1 39.2 %convolution_bitcast_fusion.1 = f32[2048,128]{0,1:T(8,128)S(1)} fusion(f32[4096,128]{1,0:T(8,128)} %all-gather.9.cloned.1.call-done, f32[2048,4096]{1,0:T(8,128)} %bitcast.37), kind=kOutput, calls=%fused_computation.1 | convolution fusion | flops 12884901888 | bytes 36700160 | tf_op jit(solution)/shard_map/dot_general | solution.py:28
  293.3 0.3 copy.18
  293.6 1.3 fusion.7
  294.9 0.0 all-gather.11.cloned.1.call-update
  295.6 54.5 %all-gather.11.cloned.1.call-done = f32[4096,128]{1,0:T(8,128)} async-done(((f32[128,128]{1,0:T(8,128)}), f32[4096,128]{1,0:T(8,128)}) %all-gather.11.cloned.1.call-update) | async-done | bytes 2097168 | tf_op jit(solution)/shard_map/all_gather | solution.py:27
  350.2 39.2 %convolution_bitcast_fusion = f32[2048,128]{0,1:T(8,128)S(1)} fusion(f32[4096,128]{1,0:T(8,128)} %all-gather.11.cloned.1.call-done, f32[2048,4096]{1,0:T(8,128)} %bitcast.38), kind=kOutput, calls=%fused_computation | convolution fusion | flops 12884901888 | bytes 36700160 | tf_op jit(solution)/shard_map/dot_general | solution.py:28
  389.4 0.0 copy-start.1
  389.4 0.0 copy-start.2
  389.4 0.0 copy-start.3
  389.4 0.0 copy-start.4
  389.4 0.3 copy.21
  389.8 0.7 fusion.5
  390.5 0.0 copy-done.1
  390.5 0.0 copy-done.2
  390.5 0.0 copy-done.3
  390.5 0.0 copy-done.4
  390.6 38.5 %all-reduce = (f32[128]{0:T(128)S(1)}, f32[4,128]{1,0:T(4,128)S(1)}, f32[4,128]{1,0:T(4,128)}) all-reduce(f32[128]{0:T(128)S(1)} %fusion.10, f32[4,128]{1,0:T(4,128)S(1)} %get-tuple-element.20, f32[4,128]{1,0:T(4,128)S(1)} %get-tuple-element.21), channel_id=1, replica_groups=mesh['state'=32] {'state'}, use_global_device_ids=true, to_apply=%region_4.5 | all-reduce | flops 1152 | bytes 9216 | tf_op jit(solution)/shard_map/pmax | solution.py:43
  429.1 0.6 broadcast_subtract_fusion
  429.7 0.6 neg.7
  (3 shorter events, 0.1 us)
Async XLA Ops:
  7.2 62.6 %all-gather.5.cloned.1.call-start = ((), (), s32[]{:S(2)}) async-start(), calls=%async_computation | async-start | bytes 2162688 | tf_op jit(solution)/shard_map/all_gather | solution.py:27
  7.9 150.1 %all-gather.7.cloned.1.call-start = ((), (), s32[]{:S(2)}) async-start(), calls=%async_computation.1 | async-start | bytes 2162688 | tf_op jit(solution)/shard_map/all_gather | solution.py:27
  8.6 92.8 %copy-start = (f32[128,16,128]{2,1,0:T(8,128)S(1)}, f32[128,16,128]{2,1,0:T(8,128)}, u32[]{:S(2)}) copy-start(f32[128,16,128]{2,1,0:T(8,128)} %param.6) | copy-start | bytes 3145732
  102.8 151.3 %all-gather.9.cloned.1.call-start = ((), (), s32[]{:S(2)}) async-start(), calls=%async_computation.2 | async-start | bytes 2162688 | tf_op jit(solution)/shard_map/all_gather | solution.py:27
  198.9 151.3 %all-gather.11.cloned.1.call-start = ((), (), s32[]{:S(2)}) async-start(), calls=%async_computation.3 | async-start | bytes 2162688 | tf_op jit(solution)/shard_map/all_gather | solution.py:27
  389.4 1.1 copy-start.1
  389.4 1.1 copy-start.2
  389.4 1.1 copy-start.3
  389.4 1.1 copy-start.4
Sparse Core Ops, SparseCore 0:
  10.8 58.9 all-gather.4
  102.9 55.0 all-gather.6
  199.0 55.0 all-gather.8
  295.1 55.0 all-gather.10
where the time goes:
time: 437 us
  waiting for transfers between devices  226 us (52%)
  matrix products  149 us (34%)
  blocking collectives  38.5 us (9%)
  between operations  14.6 us (3%)
  other arithmetic  6.59 us (2%)
    all_gather x4, waiting for transfers between devices, local(): field_all = lax.all_gather(unshifted, 'state', axis=0, tiled=True)  226 us
    dot_general x4, matrix products, local(): jnp.dot(flat_rows, field_all, precision=lax.Precision.HIGHEST, preferred_...  149 us
    pmax x1, blocking collectives, local(): lax.pmax((masked_row, jnp.stack(upper_list), -jnp.stack(lower_list)), 'st...  38.5 us
  transfers between devices with their start and end apart: 4, of which 4 were waited for; matrix products, arithmetic and copies ran while one was open for 0% of the time, Pallas kernels for 0%

commit v1 on v0

v1 whole, which is shorter than its diff:
```python
import functools

import jax
import jax.numpy as jnp
from jax import lax
from jax.experimental import pallas as pl
from jax.experimental.pallas import tpu as pltpu
from jax.sharding import PartitionSpec as P

ITERS = 4
PLANE = 8
MESH = pl.DeviceIdType.MESH

big_value = 1e30


def kernel(
    n, vc_ref, ref_ref, p_hbm, cost_hbm, start_hbm,
    rel_ref, low_ref, up_ref,
    field, pmat, wmat, acc, costs, stage, sbuf, rbuf,
    stage_sem, in_sem, send_sem, recv_sem, rsend_sem, rrecv_sem,
):
    planes = n // PLANE
    local, scen = start_hbm.shape
    rows, states = p_hbm.shape
    actions = rows // local
    kp = states // planes
    slots, chunk = stage.shape[0], stage.shape[1]
    chunks = rows // chunk
    me = lax.axis_index("state")
    z, low, core = me // PLANE, me % PLANE, me % 2
    dp = 1 - 2 * core
    dx = 2 - 4 * ((me // 2) % 2)
    dy = 4 - 8 * ((me // 4) % 2)
    da = dx + core * (dy - dx)
    db = dy + core * (dx - dy)

    def load(c):
        slot = lax.rem(c, slots)
        return pltpu.make_async_copy(
            p_hbm.at[pl.ds(c * chunk, chunk)], stage.at[slot], stage_sem.at[slot]
        )

    start_copy = pltpu.make_async_copy(start_hbm, field.at[0, me], in_sem.at[0])
    cost_copy = pltpu.make_async_copy(cost_hbm, costs, in_sem.at[1])
    start_copy.start()
    for c in range(slots):
        load(c).start()
    cost_copy.start()

    barrier = pltpu.get_barrier_semaphore()
    for delta in (dp, da, db):
        pl.semaphore_signal(barrier, inc=1, device_id=(me + delta,), device_id_type=MESH)

    def greet(d, carry):
        pl.semaphore_signal(
            barrier, inc=1, device_id=(lax.rem(z + d, planes) * PLANE + low,), device_id_type=MESH
        )
        return carry

    lax.fori_loop(1, planes, greet, 0)
    pl.semaphore_wait(barrier, 3 + planes - 1)

    def copy(it, slot, kind, d, target):
        return pltpu.make_async_remote_copy(
            src_ref=field.at[it, slot],
            dst_ref=field.at[it, slot],
            send_sem=send_sem.at[kind, d],
            recv_sem=recv_sem.at[it % 2, slot],
            device_id=(target,),
            device_id_type=MESH,
        )

    def column(d):
        return lax.rem(z + planes - d, planes) * PLANE + low

    def arrived(it, slot):
        copy(it, slot, 0, 0, me + dp).wait_recv()

    def spread(it, d):
        col = column(d)
        copy(it, col, 1, d, me + da).start()
        copy(it, col, 2, d, me + db).start()
        copy(it, col, 0, d, me + dp).start()

    def own_sends(it):
        def line(d, carry):
            copy(it, me, 7, d, lax.rem(z + d, planes) * PLANE + low).start()
            return carry

        spread(it, 0)
        lax.fori_loop(1, planes, line, 0)

    def from_line(it, d):
        arrived(it, column(d))
        spread(it, d)

    def across(it, d):
        col = column(d)
        arrived(it, col + db)
        copy(it, col + db, 3, d, me + da).start()
        copy(it, col + db, 4, d, me + dp).start()
        arrived(it, col + da)
        copy(it, col + da, 5, d, me + dp).start()

    def sends_done(it):
        def one(d, carry):
            for kind in range(7):
                copy(it, me, kind, d, me + dp).wait_send()
            return carry

        def line(d, carry):
            copy(it, me, 7, d, me + dp).wait_send()
            return carry

        lax.fori_loop(0, planes, one, 0)
        lax.fori_loop(1, planes, line, 0)

    tile = min(512, rows)

    def multiply(it, d):
        col = column(d)
        plane = col // PLANE
        arrived(it, col + da + db)
        copy(it, col + da + db, 6, d, me + dp).start()
        for delta in (0, da, db, da + db):
            arrived(it, col + dp + delta)
        for part in range(PLANE):
            v = field[it, plane * PLANE + part]
            hi = v.astype(jnp.bfloat16)
            lo = (v - hi.astype(jnp.float32)).astype(jnp.bfloat16)
            for half in range(2):
                at = half * kp + part * local
                wmat[at : at + local, :scen] = hi
                wmat[at : at + local, scen:] = lo

        @pl.loop(0, rows // tile)
        def _(m):
            at = pl.ds(pl.multiple_of(m * tile, tile), tile)
            out = jnp.dot(pmat[plane, at, :], wmat[...], preferred_element_type=jnp.float32)
            acc[at, :] += out[:, :scen] + out[:, scen:]

    group = min(16, local)

    def finish(it):
        @pl.loop(0, local // group)
        def _(g):
            at = pl.ds(pl.multiple_of(g * group * actions, group * actions), group * actions)
            q = acc[at, :].reshape(group, actions, scen)
            rel_ref[pl.ds(pl.multiple_of(g * group, group), group), :] = jnp.min(q, axis=1)

        best = rel_ref[...]

        if not isinstance(it, int) or it < ITERS - 1:
            @pl.when(it < ITERS - 1)
            def _():
                field[it + 1, me] = best

        increase = best - field[it, me]
        sbuf[0, pl.ds(it, 1), :] = jnp.max(increase, axis=0, keepdims=True)
        sbuf[0, pl.ds(ITERS + it, 1), :] = -jnp.min(increase, axis=0, keepdims=True)
        acc[...] = costs[...]

    sbuf[0] = jnp.full(sbuf.shape[1:], -big_value, jnp.float32)
    start_copy.wait()
    own_sends(0)

    def convert(c, carry):
        load(c).wait()
        slot = lax.rem(c, slots)

        @pl.loop(0, chunk // 16)
        def _(r):
            src = pl.ds(pl.multiple_of(r * 16, 16), 16)
            dst = pl.ds(pl.multiple_of(c * chunk + r * 16, 16), 16)
            for plane in range(planes):
                x = stage[slot, src, plane * kp : (plane + 1) * kp]
                hi = x.astype(jnp.bfloat16)
                pmat[plane, dst, :kp] = hi
                pmat[plane, dst, kp:] = (x - hi.astype(jnp.float32)).astype(jnp.bfloat16)

        @pl.when(c + slots < chunks)
        def _():
            load(c + slots).start()

        return carry

    def each(begin, end, step, it):
        def one(d, carry):
            step(it, d)
            return carry

        lax.fori_loop(begin, end, one, 0)

    lax.fori_loop(0, chunks // 2, convert, 0)
    each(1, planes, from_line, 0)
    across(0, 0)
    lax.fori_loop(chunks // 2, 3 * chunks // 4, convert, 0)
    each(1, planes, across, 0)
    lax.fori_loop(3 * chunks // 4, chunks, convert, 0)

    cost_copy.wait()

    @pl.loop(0, local)
    def _(s):
        at = pl.ds(pl.multiple_of(s * actions, actions), actions)
        allowed = lax.broadcasted_iota(jnp.int32, (actions, scen), 0) < vc_ref[s]
        masked = jnp.where(allowed, costs[at, :], jnp.float32(big_value))
        costs[at, :] = masked
        acc[at, :] = masked

    each(0, planes, multiply, 0)
    finish(0)
    sends_done(0)

    def iteration(it, carry):
        own_sends(it)

        def step(d, carry):
            @pl.when(jnp.logical_and(d >= 1, d < planes))
            def _():
                from_line(it, d)

            @pl.when(jnp.logical_and(d >= 1, d < planes + 1))
            def _():
                across(it, d - 1)

            @pl.when(d >= 2)
            def _():
                multiply(it, d - 2)

            return carry

        lax.fori_loop(1, planes + 2, step, 0)
        finish(it)
        sends_done(it)
        return carry

    lax.fori_loop(1, ITERS, iteration, 0)

    position = lax.broadcasted_iota(jnp.int32, (local, scen), 0) + me * local
    chosen = jnp.where(position == ref_ref[0], rel_ref[...], jnp.float32(-big_value))
    sbuf[0, 2 * ITERS : 2 * ITERS + 1, :] = jnp.max(chosen, axis=0, keepdims=True)

    def reduce_copy(source, slot, target):
        return pltpu.make_async_remote_copy(
            src_ref=sbuf.at[source],
            dst_ref=rbuf.at[slot],
            send_sem=rsend_sem.at[slot],
            recv_sem=rrecv_sem.at[slot],
            device_id=(target,),
            device_id_type=MESH,
        )

    for number, delta in enumerate((dp, da, db)):
        step = reduce_copy(number, number, me + delta)
        step.start()
        step.wait_recv()
        sbuf[number + 1] = jnp.maximum(sbuf[number], rbuf[number])
        step.wait_send()

    def along(d):
        return reduce_copy(3, 2 + d, lax.rem(z + d, planes) * PLANE + low)

    def send(d, carry):
        along(d).start()
        return carry

    def take(d, total):
        along(d).wait_recv()
        return jnp.maximum(total, rbuf[2 + d])

    def sent(d, carry):
        along(d).wait_send()
        return carry

    lax.fori_loop(1, planes, send, 0)
    total = lax.fori_loop(1, planes, take, sbuf[3])
    lax.fori_loop(1, planes, sent, 0)
    up_ref[...] = total[:ITERS]
    low_ref[...] = -total[ITERS : 2 * ITERS]
    rel_ref[...] = rel_ref[...] - total[2 * ITERS : 2 * ITERS + 1]


def solution(mesh):
    n = mesh.shape["state"]

    def local_step(transitions, costs, valid_counts, start_values, ref_state):
        local, actions, states = transitions.shape
        scen = start_values.shape[1]
        rows = local * actions
        planes = n // PLANE
        kp = states // planes
        chunk = min(64, rows // 4)
        slots = min(8, rows // chunk)
        f32, bf16 = jnp.float32, jnp.bfloat16
        vmem = pl.BlockSpec(memory_space=pltpu.VMEM)
        smem = pl.BlockSpec(memory_space=pltpu.SMEM)
        hbm = pl.BlockSpec(memory_space=pl.ANY)
        rel, low, up = pl.pallas_call(
            functools.partial(kernel, n),
            out_shape=(
                jax.ShapeDtypeStruct((local, scen), f32),
                jax.ShapeDtypeStruct((ITERS, scen), f32),
                jax.ShapeDtypeStruct((ITERS, scen), f32),
            ),
            in_specs=[smem, smem, hbm, hbm, hbm],
            out_specs=(vmem, vmem, vmem),
            scratch_shapes=[
                pltpu.VMEM((ITERS, n, local, scen), f32),
                pltpu.VMEM((planes, rows, 2 * kp), bf16),
                pltpu.VMEM((2 * kp, 2 * scen), bf16),
                pltpu.VMEM((rows, scen), f32),
                pltpu.VMEM((rows, scen), f32),
                pltpu.VMEM((slots, chunk, states), f32),
                pltpu.VMEM((4, 16, scen), f32),
                pltpu.VMEM((2 + planes, 16, scen), f32),
                pltpu.SemaphoreType.DMA((slots,)),
                pltpu.SemaphoreType.DMA((2,)),
                pltpu.SemaphoreType.DMA((8, planes)),
                pltpu.SemaphoreType.DMA((2, n)),
                pltpu.SemaphoreType.DMA((2 + planes,)),
                pltpu.SemaphoreType.DMA((2 + planes,)),
            ],
            compiler_params=pltpu.CompilerParams(
                collective_id=0, has_side_effects=True, vmem_limit_bytes=66 * 1000 * 1000
            ),
        )(
            valid_counts, ref_state, transitions.reshape(rows, states),
            costs.reshape(rows, scen), start_values,
        )
        return rel, low, up

    in_specs = (P("state", None, None), P("state", None, None), P("state"), P("state", None), P())
    out_specs = (P("state", None), P(), P())
    return jax.shard_map(local_step, mesh=mesh, in_specs=in_specs, out_specs=out_specs, check_vma=False)
```

time: 437 us -> 133 us (0.30)
  waiting for transfers between devices: 226 us -> 0 us
  matrix products: 149 us -> 0 us
  Pallas kernels: 0 us -> 127 us
  blocking collectives: 38.5 us -> 0 us
  between operations: 14.6 us -> 1.29 us
  other arithmetic: 6.59 us -> 0 us
    all_gather x4 -> x0, waiting for transfers between devices: 226 us -> none  [local(): field_all = lax.all_gather(unshifted, 'state', axis=0, tiled=True)]
    dot_general x4 -> x0, matrix products: 149 us -> none  [local(): jnp.dot(flat_rows, field_all, precision=lax.Precision.HIGHEST, preferred_...]
    pallas_call x0 -> x1, Pallas kernels: none -> 127 us  [local_step(): pl.pallas_call(functools.partial(kernel, n), out_shape=(jax.ShapeDtypeStr...]
    pmax x1 -> x0, blocking collectives: 38.5 us -> none  [local(): lax.pmax((masked_row, jnp.stack(upper_list), -jnp.stack(lower_list)), 'st...]
    reduce_min x4 -> x0, other arithmetic: 4.64 us -> none  [local(): best_value = jnp.min(q_values, axis=1)]
  transfers between devices with their start and end apart: 4 -> 0, of which waited for: 4 -> 0; matrix products, arithmetic and copies ran while one was open for 0% -> 0% of each run, Pallas kernels for 0% -> 0%
where the time goes in v1:
time: 133 us
  Pallas kernels  127 us (95%)
  local copies, waits for them, and re-layouts  3.98 us (3%)
    pallas_call x1, Pallas kernels, local_step(): pl.pallas_call(functools.partial(kernel, n), out_shape=(jax.ShapeDtypeStr...  127 us
    unnamed x3, local copies, waits for them, and re-layouts  3.98 us

profile of v1, /device:TPU:0, one launch (start us, length us, event | category | flops | bytes accessed | tf_op | source)
XLA Modules:
  0.0 132.6 jit_solution(8057365369540003391)
XLA Ops:
  1.3 127.3 %shard_map.76 = (f32[128,128]{1,0:T(8,128)}, f32[4,128]{1,0:T(4,128)}, f32[4,128]{1,0:T(4,128)}) custom-call(s32[128]{0:T(128)} %vc_ref.1, s32[1]{0:T(128)S(6)} %copy.11.ref_ref, f32[2048,4096]{1,0:T(8,128)} %bitcast.2, f32[2048,128]{1,0:T(8,128)} %bitcast.3, f32[128,128]{1,0:T(8,128)} %start_hbm.1), custom_call_target="tpu_custom_call" | custom-call | tf_op jit(solution)/shard_map/pallas_call | solution.py:300
  128.6 1.5 %copy.12 = f32[128,128]{1,0:T(8,128)} copy(f32[128,128]{1,0:T(8,128)} %get-tuple-element.6) | data formatting | bytes 131072
  130.1 1.2 copy.13
  131.3 1.3 copy.14
